TPU v7x, 128 devices: a whole 4x4x4 slice. The times are simulated.
128 devices in a mesh: section: 2 (over core), tp: 8 (over z_lo, x), fsdp: 8 (over z_hi, y).
Axes of the slice: x: 4, y: 4, z: 4 (z_hi: 2, z_lo: 2; z = z_hi * 2 + z_lo), core: 2. Of those that a mesh axis runs over, the one named last changes fastest.
Arguments:
- normed: bfloat16 [2, 1024, 4608], P('section', 'tp', 'fsdp'), may hold values from -6 to 6
- cotangent: bfloat16 [2, 1024, 4608], P('section', 'tp', 'fsdp'), may hold values from -6 to 6
- w_gate: bfloat16 [2, 4608, 18432], P('section', 'fsdp', 'tp'), may hold values from -0.09375 to 0.09375
- w_up: bfloat16 [2, 4608, 18432], P('section', 'fsdp', 'tp'), may hold values from -0.09375 to 0.09375
- w_down: bfloat16 [2, 4608, 18432], P('section', 'fsdp', 'tp'), may hold values from -0.046875 to 0.046875
Outputs:
- passed: bfloat16 [2, 1024, 4608], P('section', 'tp', 'fsdp')
- grad_gate: bfloat16 [2, 4608, 18432], P('section', 'fsdp', 'tp')
- grad_up: bfloat16 [2, 4608, 18432], P('section', 'fsdp', 'tp')
- grad_down: bfloat16 [2, 4608, 18432], P('section', 'fsdp', 'tp')
All inputs are finite; a program needn't handle non-finite values.
Results may differ from a plain program's by a relative error of at most 0.012.
Values may be sent and summed in bfloat16 or wider, within the bound.
No kernel may reach another device: no remote copies, remote signals or barrier semaphores. Data moves between devices by JAX's collectives and lax.ppermute only.
A program may use at most 192 MiB of HBM per device.

v0:
```python
import math

import jax
import jax.numpy as jnp
from jax import lax
from jax.sharding import PartitionSpec as P


def from_everyone(x, axis):
    copies = jnp.broadcast_to(x, (lax.axis_size(axis), *x.shape))
    return lax.all_to_all(copies, axis, split_axis=0, concat_axis=0, tiled=True)


def laid_out(parts, dim):
    parts = jnp.moveaxis(parts, 0, dim)
    lengths = parts.shape
    return parts.reshape(*lengths[:dim], lengths[dim] * lengths[dim + 1], *lengths[dim + 2 :])


def gathered_copies(x, axis, dim):
    parts = from_everyone(x, axis)
    return laid_out(parts, dim)


def sent_together(arrays, axis, dim, along):
    ends, at = ([], 0)
    for a in arrays[:-1]:
        at += a.shape[along]
        ends.append(at)
    both = jnp.concatenate(arrays, axis=along)
    return tuple(jnp.split(gathered_copies(both, axis, dim), ends, axis=along))


def in_one_piece(arrays, axis, dim, along):
    ends, at = ([], 0)
    for a in arrays[:-1]:
        at += a.shape[along]
        ends.append(at)
    both = jnp.concatenate(arrays, axis=along)
    return tuple(jnp.split(lax.all_gather(both, axis, axis=dim, tiled=True), ends, axis=along))


def in_blocks(x, dim, length):
    lengths = x.shape
    parts = x.reshape(*lengths[:dim], length, lengths[dim] // length, *lengths[dim + 1 :])
    return jnp.moveaxis(parts, dim, 0)


def summed_on_arrival(x, axis, dim):
    parts = in_blocks(x, dim, lax.axis_size(axis))
    arrived = lax.all_to_all(parts, axis, split_axis=0, concat_axis=0, tiled=True)
    return arrived.astype(jnp.float32).sum(axis=0)


def from_behind(value, axis, steps):
    count = lax.axis_size(axis)
    pairs = [(source, (source + steps) % count) for source in range(count)]
    return lax.ppermute(value, axis, pairs)


def activate(gate, up, back):
    coeff = math.sqrt(2.0 / math.pi)
    inner = jnp.tanh(coeff * (gate + 0.044715 * gate * gate * gate))
    act = 0.5 * gate * (1.0 + inner)
    slope = 0.5 * (1.0 + inner) + 0.5 * gate * (1.0 - inner * inner) * coeff * (
        1.0 + 3.0 * 0.044715 * gate * gate
    )
    hidden = (act * up).astype(jnp.bfloat16)
    d_gate = (back * up * slope).astype(jnp.bfloat16)
    d_up = (back * act).astype(jnp.bfloat16)
    return (hidden, d_gate, d_up)


def column_grad(left, right):
    return lax.dot_general(
        left, right, (((0,), (0,)), ((), ())), preferred_element_type=jnp.float32
    )


def row_back(grads, weight):
    return lax.dot_general(
        grads, weight, (((1,), (1,)), ((), ())), preferred_element_type=jnp.float32
    )


def local(normed, cotangent, w_gate, w_up, w_down):
    rows_own = normed[0]
    cot_own = cotangent[0]
    wgate = w_gate[0]
    wup = w_up[0]
    wdown = w_down[0]
    rows_all, cot_all = sent_together((rows_own, cot_own), "tp", 0, 1)
    total = rows_all.shape[0]
    width = wgate.shape[1]
    scale = 1.0 / math.sqrt(total)
    gate = jnp.dot(rows_all, wgate, preferred_element_type=jnp.float32)
    up = jnp.dot(rows_all, wup, preferred_element_type=jnp.float32)
    back = jnp.dot(cot_all, wdown, preferred_element_type=jnp.float32)
    summed = lax.psum_scatter(
        jnp.concatenate((gate, up, back), axis=1), "fsdp", scatter_dimension=0, tiled=True
    )
    part_hidden, part_gate, part_up = activate(
        summed[:, :width], summed[:, width : 2 * width], summed[:, 2 * width :]
    )
    hidden, d_gate, d_up = in_one_piece((part_hidden, part_gate, part_up), "fsdp", 0, 1)
    grad_gate = (column_grad(rows_all, d_gate) * scale).astype(jnp.bfloat16)
    grad_up = (column_grad(rows_all, d_up) * scale).astype(jnp.bfloat16)
    grad_down = (column_grad(cot_all, hidden) * scale).astype(jnp.bfloat16)
    branch = summed_on_arrival(
        (row_back(d_gate, wgate) + row_back(d_up, wup)).astype(jnp.bfloat16), "tp", 0
    )
    handed = (cot_own.astype(jnp.float32) + branch).astype(jnp.bfloat16)
    passed = from_behind(handed, "section", 1)
    return (passed[None], grad_gate[None], grad_up[None], grad_down[None])


def solution(mesh):
    in_specs = (
        P("section", "tp", "fsdp"),
        P("section", "tp", "fsdp"),
        P("section", "fsdp", "tp"),
        P("section", "fsdp", "tp"),
        P("section", "fsdp", "tp"),
    )
    out_specs = (
        P("section", "tp", "fsdp"),
        P("section", "fsdp", "tp"),
        P("section", "fsdp", "tp"),
        P("section", "fsdp", "tp"),
    )
    return jax.shard_map(local, mesh=mesh, in_specs=in_specs, out_specs=out_specs, check_vma=False)
```

profile of v0, /device:TPU:1, one launch (start us, length us, event | category | flops | bytes accessed | tf_op | source)
XLA Modules:
  0.0 590.9 jit_solution(10289725890272365546)
XLA Ops:
  7.2 0.0 copy-start
  7.2 0.0 reduce-scatter.2.cloned.1.call-start
  7.2 1.2 pad_maximum_fusion.2
  8.4 0.2 copy.10
  8.6 0.3 broadcast_in_dim.15
  8.9 34.9 %all_to_all.10 = bf16[8,128,1152]{2,1,0:T(8,128)(2,1)S(1)} all-to-all(bf16[8,128,1152]{2,1,0:T(8,128)(2,1)S(1)} %broadcast_in_dim.15), channel_id=1, replica_groups=mesh['section'=2,'tp'=8,'fsdp'=8] {'tp'}, dimensions={0} | all-to-all | bytes 4718592 | tf_op jit(solution)/shard_map/all_to_all | solution.py:11
  43.8 6.2 %fusion.15 = f32[1024,2304]{1,0:T(8,128)} fusion(bf16[1,576,2304]{2,1,0:T(8,128)(2,1)S(1)} %copy-done, bf16[1024,1152]{1,0:T(8,128)(2,1)S(1)} %bitcast.34), kind=kOutput, calls=%fused_computation.17 | convolution fusion | flops 2717908992 | bytes 13402112 | tf_op jit(solution)/shard_map/dot_general | solution.py:97
  50.1 6.4 %fusion.12 = f32[1024,2304]{1,0:T(8,128)} fusion(bf16[1,576,2304]{2,1,0:T(8,128)(2,1)S(1)} %copy-done.4, bf16[1024,1152]{1,0:T(8,128)(2,1)S(1)} %bitcast.35), kind=kOutput, calls=%fused_computation.14 | convolution fusion | flops 2717908992 | bytes 13402112 | tf_op jit(solution)/shard_map/dot_general | solution.py:98
  56.5 0.0 copy-done.5
  56.5 6.1 %fusion.18 = f32[1024,2304]{1,0:T(8,128)} fusion(bf16[1,576,2304]{2,1,0:T(8,128)(2,1)S(1)} %copy-done.5, bf16[1024,1152]{1,0:T(8,128)(2,1)S(1)} %bitcast.36), kind=kOutput, calls=%fused_computation.20 | convolution fusion | flops 2717908992 | bytes 13402112 | tf_op jit(solution)/shard_map/dot_general | solution.py:96
  62.6 20.3 %pad_maximum_fusion = f32[1024,6912]{1,0:T(8,128)} fusion(f32[1024,2304]{1,0:T(8,128)} %fusion.12, f32[1024,2304]{1,0:T(8,128)} %fusion.15, f32[1024,2304]{1,0:T(8,128)} %fusion.18), kind=kLoop, calls=%fused_computation | loop fusion | flops 14155776 | bytes 56623104 | tf_op jit(solution)/shard_map/concatenate | solution.py:100
  82.8 0.0 reduce-scatter.2.cloned.1.call-update
  82.9 0.0 all-gather.2.cloned.1.call-start
  82.9 293.2 %reduce-scatter.2.cloned.1.call-done = f32[128,6912]{1,0:T(8,128)} async-done(((f32[1024,6912]{1,0:T(8,128)}), f32[128,6912]{1,0:T(8,128)}) %reduce-scatter.2.cloned.1.call-update) | async-done | bytes 3538960 | tf_op jit(solution)/shard_map/reduce_scatter | solution.py:99
  376.1 2.9 multiply_convert_fusion.4
  379.1 1.3 pad_maximum_fusion.1
  380.4 0.0 all-gather.2.cloned.1.call-update
  380.4 160.1 %all-gather.2.cloned.1.call-done = bf16[1024,6912]{1,0:T(8,128)(2,1)} async-done(((bf16[128,6912]{1,0:T(8,128)(2,1)}), bf16[1024,6912]{1,0:T(8,128)(2,1)}) %all-gather.2.cloned.1.call-update) | async-done | bytes 14155792 | tf_op jit(solution)/shard_map/all_gather | solution.py:40
  540.5 5.0 fusion.7
  545.5 5.3 fusion.24
  550.8 1.2 copy.14
  552.0 4.4 all-to-all-start.1
  556.5 0.0 copy-start.2
  556.5 7.3 %fusion.1 = bf16[1,576,2304]{2,1,0:T(8,128)(2,1)} fusion(bf16[1024,6912]{1,0:T(8,128)(2,1)} %all-gather.2.cloned.1.call-done, bf16[1024,1152]{1,0:T(8,128)(2,1)} %bitcast.37), kind=kOutput, calls=%fused_computation.5 | convolution fusion | flops 2720563200 | bytes 8683520 | tf_op jit(solution)/shard_map/dot_general | solution.py:75
  563.8 6.9 %fusion.2 = bf16[1,576,2304]{2,1,0:T(8,128)(2,1)} fusion(bf16[1024,6912]{1,0:T(8,128)(2,1)} %all-gather.2.cloned.1.call-done, bf16[1024,1152]{1,0:T(8,128)(2,1)S(1)} %bitcast.39), kind=kOutput, calls=%fused_computation.6 | convolution fusion | flops 2720563200 | bytes 8683520 | tf_op jit(solution)/shard_map/dot_general | solution.py:75
  570.7 2.9 all-to-all-done.1
  573.6 1.5 convert_reduce_fusion
  575.1 0.0 copy-done.3
  575.1 0.9 collective-permute-start
  576.0 7.4 %fusion.3 = bf16[1,576,2304]{2,1,0:T(8,128)(2,1)} fusion(bf16[1024,6912]{1,0:T(8,128)(2,1)} %all-gather.2.cloned.1.call-done, bf16[1024,1152]{1,0:T(8,128)(2,1)} %bitcast.38), kind=kOutput, calls=%fused_computation.7 | convolution fusion | flops 2720563200 | bytes 8683520 | tf_op jit(solution)/shard_map/dot_general | solution.py:75
  583.4 0.0 collective-permute-done
  583.4 0.7 copy.16
  (11 shorter events, 0.1 us)
Async XLA Ops:
  7.2 36.7 %copy-start = (bf16[1,576,2304]{2,1,0:T(8,128)(2,1)S(1)}, bf16[1,576,2304]{2,1,0:T(8,128)(2,1)}, u32[]{:S(2)}) copy-start(bf16[1,576,2304]{2,1,0:T(8,128)(2,1)} %param.8) | copy-start | bytes 7962628
  7.2 369.0 %reduce-scatter.2.cloned.1.call-start = ((), (), s32[]{:S(2)}) async-start(), calls=%async_computation.3 | async-start | bytes 31850496 | tf_op jit(solution)/shard_map/reduce_scatter | solution.py:99
  43.8 12.6 %copy-start.1 = (bf16[8,128,1152]{2,1,0:T(8,128)(2,1)}, bf16[8,128,1152]{2,1,0:T(8,128)(2,1)S(1)}, u32[]{:S(2)}) copy-start(bf16[8,128,1152]{2,1,0:T(8,128)(2,1)S(1)} %all_to_all.10) | copy-start | bytes 7077892
  43.8 6.2 %copy-start.4 = (bf16[1,576,2304]{2,1,0:T(8,128)(2,1)S(1)}, bf16[1,576,2304]{2,1,0:T(8,128)(2,1)}, u32[]{:S(2)}) copy-start(bf16[1,576,2304]{2,1,0:T(8,128)(2,1)} %param.9) | copy-start | bytes 7962628
  50.1 6.4 %copy-start.5 = (bf16[1,576,2304]{2,1,0:T(8,128)(2,1)S(1)}, bf16[1,576,2304]{2,1,0:T(8,128)(2,1)}, u32[]{:S(2)}) copy-start(bf16[1,576,2304]{2,1,0:T(8,128)(2,1)} %param.7) | copy-start | bytes 7962628
  82.9 457.7 %all-gather.2.cloned.1.call-start = ((), (), s32[]{:S(2)}) async-start(), calls=%async_computation.4 | async-start | bytes 15925248 | tf_op jit(solution)/shard_map/all_gather | solution.py:40
  540.5 5.0 copy-start.6
  552.0 21.6 %all-to-all-start.1 = ((bf16[8,128,576]{1,2,0:T(8,128)(2,1)}), bf16[8,128,576]{1,2,0:T(8,128)(2,1)}, u32[]{:S(2)}, u32[]{:S(2)}) async-start(bf16[8,128,576]{1,2,0:T(8,128)(2,1)} %bitcast.33), calls=%async_computation.2 | async-start | bytes 2359296 | tf_op jit(solution)/shard_map/all_to_all | solution.py:51
  556.5 7.4 %copy-start.2 = (bf16[8,128,1152]{2,1,0:T(8,128)(2,1)S(1)}, bf16[8,128,1152]{2,1,0:T(8,128)(2,1)}, u32[]{:S(2)}) copy-start(bf16[8,128,1152]{2,1,0:T(8,128)(2,1)} %copy-done.1) | copy-start | bytes 7077892
  563.8 11.2 %copy-start.3 = (bf16[1,128,576]{1,2,0:T(8,128)(2,1)S(1)}, bf16[1,128,576]{1,2,0:T(8,128)(2,1)}, u32[]{:S(2)}) copy-start(bf16[1,128,576]{1,2,0:T(8,128)(2,1)} %param.6) | copy-start | bytes 442372
  575.1 8.3 %collective-permute-start = (bf16[128,576]{0,1:T(8,128)(2,1)S(1)}, bf16[128,576]{0,1:T(8,128)(2,1)S(1)}, u32[]{:S(2)}, u32[]{:S(2)}) collective-permute-start(bf16[128,576]{0,1:T(8,128)(2,1)S(1)} %add_convert_fusion.1), channel_id=1, source_target_pairs={{0,64},{64,0},{1,65},{65,1},{2,66},{66,2},{3,67},{67,3},{4,68},{68... | collective-permute-start | bytes 442376 | tf_op jit(solution)/shard_map/ppermute | solution.py:58
Sparse Core Ops, SparseCore 0:
  83.0 293.1 reduce-scatter.1
  380.5 159.9 all-gather.1
where the time goes:
time: 591 us
  waiting for transfers between devices  456 us (77%)
  matrix products  50.6 us (9%)
  blocking collectives  34.9 us (6%)
  other arithmetic  27.1 us (5%)
  between operations  14.1 us (2%)
    reduce_scatter x1, waiting for transfers between devices, local(): lax.psum_scatter(jnp.concatenate((gate, up, back), axis=1), 'fsdp', scatt...  293 us
    all_gather x1, waiting for transfers between devices, in_one_piece(): lax.all_gather(both, axis, axis=dim, tiled=True)  160 us
    all_to_all x1, blocking collectives, from_everyone(): return lax.all_to_all(copies, axis, split_axis=0, concat_axis=0, tiled=True)  34.9 us
    dot_general x3, matrix products, column_grad(): lax.dot_general(left, right, (((0,), (0,)), ((), ())), preferred_element_...  21.6 us
    concatenate x1, other arithmetic, local(): jnp.concatenate((gate, up, back), axis=1)  20.3 us
  transfers between devices with their start and end apart: 4, of which 3 were waited for; matrix products, arithmetic and copies ran while one was open for 4% of the time, Pallas kernels for 0%

commit v1 on v0

v1 whole, which is shorter than its diff:
```python
import math

import jax
import jax.numpy as jnp
from jax import lax
from jax.experimental import pallas as pl
from jax.experimental.pallas import tpu as pltpu
from jax.sharding import PartitionSpec as P

TILE = 256
ROWS = 128
PART = 16
F32 = jnp.float32
BF16 = jnp.bfloat16

ROOM = pltpu.CompilerParams(vmem_limit_bytes=16 * 1024 * 1024)


def along_ring(v, axis, step):
    pairs = [(o * 4 + i, o * 4 + (i + step) % 4) for o in range(2) for i in range(4)]
    return lax.ppermute(v, axis, pairs)


def across(v, axis):
    return lax.ppermute(v, axis, [(i, (i + 4) % 8) for i in range(8)])


def added(*parts):
    total = parts[0].astype(F32)
    for p in parts[1:]:
        total = total + p.astype(F32)
    return total


def stacked(normed, cotangent):
    def kernel(n_ref, c_ref, out, cot):
        out[0] = n_ref[...].T
        rows = c_ref[...].T
        out[1] = rows
        cot[...] = rows

    depth, rows = normed.shape
    return pl.pallas_call(
        kernel,
        out_shape=[
            jax.ShapeDtypeStruct((2, rows, depth), BF16),
            jax.ShapeDtypeStruct((rows, depth), BF16),
        ],
        compiler_params=ROOM,
        name="stacked",
    )(normed, cotangent)


def gathered(own):
    left = along_ring(own, "tp", 1)
    right = along_ring(own, "tp", -1)
    other = across(own, "tp")
    far0 = along_ring(left[:1], "tp", 1)
    far1 = along_ring(right[1:], "tp", -1)
    oleft = along_ring(other, "tp", 1)
    oright = along_ring(other, "tp", -1)
    far = jnp.concatenate((far0, far1), axis=0)
    ofar = across(far, "tp")
    return [own, right, far, left, other, oright, ofar, oleft]


def project(pieces, owner, rows, weights, blocks, first, count, tile):
    depth = weights[0].shape[0]
    fresh = pieces is not None

    def kernel(*refs):
        if fresh:
            own_ref, ins = refs[0], refs[1:9]
            wg, wu, wd, rows_ref = refs[9:13]
            outs = refs[13:]

            @pl.when(pl.program_id(0) == 0)
            def _():
                for b in range(8):
                    at = pl.multiple_of(own_ref[b] * PART, PART)
                    for p in range(8):
                        lo = b * ROWS + p * PART
                        rows_ref[:, lo : lo + PART, :] = ins[p][:, pl.ds(at, PART), :]
        else:
            rows_ref, wg, wu, wd = refs[:4]
            outs = refs[4:]
        for w, (weight, which) in enumerate(((wg, 0), (wu, 0), (wd, 1))):
            left = rows_ref[which, blocks[0] * ROWS : (blocks[-1] + 1) * ROWS]
            out = jnp.dot(left, weight[...], preferred_element_type=F32).astype(BF16)
            for i in range(len(blocks)):
                outs[i][w] = out[i * ROWS : (i + 1) * ROWS]

    wspec = pl.BlockSpec((depth, tile), lambda j, *_: (0, first + j))
    rows_spec = pl.BlockSpec((2, 8 * ROWS, depth), lambda j, *_: (0, 0, 0))
    out_shape = [jax.ShapeDtypeStruct((3, ROWS, count * tile), BF16)] * len(blocks)
    out_specs = [pl.BlockSpec((3, ROWS, tile), lambda j, *_: (0, 0, j))] * len(blocks)
    if fresh:
        in_specs = [pl.BlockSpec((2, ROWS, depth), lambda j, *_: (0, 0, 0))] * 8 + [wspec] * 3
        out_shape = [jax.ShapeDtypeStruct((2, 8 * ROWS, depth), BF16)] + out_shape
        out_specs = [rows_spec] + out_specs
        args = (owner, *pieces, *weights)
    else:
        in_specs = [rows_spec] + [wspec] * 3
        args = (rows, *weights)
    return pl.pallas_call(
        kernel,
        out_shape=out_shape,
        grid_spec=pltpu.PrefetchScalarGridSpec(
            num_scalar_prefetch=1 if fresh else 0,
            grid=(count,),
            in_specs=in_specs,
            out_specs=out_specs,
        ),
        cost_estimate=pl.CostEstimate(
            flops=2 * len(blocks) * ROWS * depth * 3 * count * tile,
            bytes_accessed=2 * 3 * count * tile * (depth + len(blocks) * ROWS),
            transcendentals=0,
        ),
        compiler_params=ROOM,
    )(*args)


def flipped(rows):
    def kernel(rows_ref, out):
        for side in range(2):
            out[side] = rows_ref[side].T

    return pl.pallas_call(
        kernel,
        out_shape=jax.ShapeDtypeStruct((2, rows.shape[2], rows.shape[1]), BF16),
        cost_estimate=pl.CostEstimate(
            flops=10**8, bytes_accessed=4 * rows.size, transcendentals=0
        ),
        compiler_params=ROOM,
        name="flip",
    )(rows)


def reduced_ring_first(p):
    r1 = along_ring(p[2][1], "fsdp", 1)
    r0 = along_ring(p[2][0], "fsdp", -1)
    d1 = along_ring(p[3][1], "fsdp", -1)
    d0 = along_ring(p[1][0], "fsdp", 1)
    m1 = along_ring(added(p[1][1], r1).astype(BF16), "fsdp", 1)
    m0 = along_ring(added(p[3][0], r0).astype(BF16), "fsdp", -1)
    z = across(added(p[0][1], d1, m1).astype(BF16), "fsdp")
    return added(p[0][0], d0, m0, z)


def reduced_pair_first(p):
    half = p[0][0].shape[1] // 2
    z = {k: across(p[k][1], "fsdp") for k in (2, 1, 3, 0)}

    def low(k, *more):
        return added(p[k][0][:, :half], z[k][:, :half], *more).astype(BF16)

    def high(k, *more):
        return added(p[k][0][:, half:], z[k][:, half:], *more).astype(BF16)

    ra = along_ring(low(2), "fsdp", 1)
    rb = along_ring(high(2), "fsdp", -1)
    db = along_ring(high(1), "fsdp", 1)
    da = along_ring(low(3), "fsdp", -1)
    ma = along_ring(low(1, ra), "fsdp", 1)
    mb = along_ring(high(3, rb), "fsdp", -1)
    return added(p[0][0], z[0]) + jnp.concatenate((added(da, ma), added(db, mb)), axis=1)


def activate(sums):
    gate, up, back = sums[0], sums[1], sums[2]
    coeff = math.sqrt(2.0 / math.pi)
    inner = jnp.tanh(coeff * (gate + 0.044715 * gate * gate * gate))
    act = 0.5 * gate * (1.0 + inner)
    slope = 0.5 * (1.0 + inner) + 0.5 * gate * (1.0 - inner * inner) * coeff * (
        1.0 + 3.0 * 0.044715 * gate * gate
    )
    hidden = (act * up).astype(BF16)
    d_gate = (back * up * slope).astype(BF16)
    d_up = (back * act).astype(BF16)
    return jnp.stack((hidden, d_gate, d_up))


def spread_pair_first(own):
    z = across(own, "fsdp")
    fm = along_ring(own, "fsdp", 1)
    fp = along_ring(own, "fsdp", -1)
    gp = along_ring(z, "fsdp", -1)
    gm = along_ring(z, "fsdp", 1)
    f2 = along_ring(fm, "fsdp", 1)
    g2 = along_ring(gp, "fsdp", -1)
    return [[own], [z], [fp], [gp], [fm], [gm], [f2], [g2]]


def spread_ring_first(own):
    half = ROWS // 2
    fm = along_ring(own, "fsdp", 1)
    fp = along_ring(own, "fsdp", -1)
    z0 = across(own, "fsdp")
    fa = along_ring(fm[:, :half], "fsdp", 1)
    fb = along_ring(fp[:, half:], "fsdp", -1)
    z1 = across(fp, "fsdp")
    z3 = across(fm, "fsdp")
    za = across(fa, "fsdp")
    zb = across(fb, "fsdp")
    return [[own], [z0], [fp], [z1], [fm], [z3], [fa, fb], [za, zb]]


def flat(blocks):
    return [p for b in blocks for p in b]


def held(weights):
    def kernel(wu, wd, out):
        for i in range(8):
            out[i] = 0

    return pl.pallas_call(
        kernel,
        out_shape=jax.ShapeDtypeStruct((8,), jnp.int32),
        in_specs=[pl.BlockSpec(memory_space=pltpu.VMEM)] * 2,
        out_specs=pl.BlockSpec(memory_space=pltpu.SMEM),
        compiler_params=ROOM,
        name="held",
    )(*weights)


def part_specs(parts):
    return [pl.BlockSpec((3, p.shape[1], TILE), lambda j: (0, 0, j)) for p in parts]


SIDES = ((1, 0), (2, 0), (0, 1))


def products(sides_ref, parts, span):
    for plane, side in SIDES:
        right = jnp.concatenate([r[plane] for r in parts], axis=0)
        yield jnp.dot(sides_ref[side, :, span], right, preferred_element_type=F32)


def weight_sums(parts, sides, count):
    depth = sides.shape[1]
    tokens = sum(p.shape[1] for p in parts)

    def kernel(sides_ref, *refs):
        for out, value in zip(refs[-3:], products(sides_ref, refs[:-3], slice(0, tokens))):
            out[...] = value

    return pl.pallas_call(
        kernel,
        out_shape=[jax.ShapeDtypeStruct((depth, count * TILE), F32)] * 3,
        grid=(count,),
        in_specs=[pl.BlockSpec(sides.shape, lambda j: (0, 0, 0))] + part_specs(parts),
        out_specs=[pl.BlockSpec((depth, TILE), lambda j: (0, j))] * 3,
        cost_estimate=pl.CostEstimate(
            flops=2 * tokens * depth * 3 * count * TILE,
            bytes_accessed=2 * 3 * count * TILE * (2 * depth + tokens),
            transcendentals=0,
        ),
        compiler_params=ROOM,
    )(sides, *parts)


def weight_grads(parts, sides, sums, first, count, columns, scale, earlier):
    depth = sides.shape[1]
    n = len(parts)
    tokens = sum(p.shape[1] for p in parts)
    span = slice(sides.shape[2] - tokens, sides.shape[2])

    def kernel(sides_ref, *refs):
        for total, out, value in zip(refs[:3], refs[-3:], products(sides_ref, refs[3 : 3 + n], span)):
            out[...] = ((total[...] + value) * scale).astype(BF16)

    more = [] if earlier is None else list(earlier)
    return pl.pallas_call(
        kernel,
        out_shape=[jax.ShapeDtypeStruct((depth, columns), BF16)] * 3,
        grid=(count,),
        in_specs=[pl.BlockSpec(sides.shape, lambda j: (0, 0, 0))]
        + [pl.BlockSpec((depth, TILE), lambda j: (0, j))] * 3
        + part_specs(parts)
        + [pl.BlockSpec(memory_space=pl.ANY)] * len(more),
        out_specs=[pl.BlockSpec((depth, TILE), lambda j: (0, first + j))] * 3,
        input_output_aliases={4 + n + i: i for i in range(len(more))},
        cost_estimate=pl.CostEstimate(
            flops=2 * tokens * depth * 3 * count * TILE,
            bytes_accessed=2 * 3 * count * TILE * (3 * depth + tokens),
            transcendentals=0,
        ),
        compiler_params=ROOM,
    )(sides, *sums, *parts, *more)


def input_grad(parts_a, parts_b, weights, n_a, n_b, earlier, final):
    depth = weights[0].shape[0]
    na, nb = len(parts_a), len(parts_b)
    rows = sum(p.shape[1] for p in parts_a)
    before = 0 if earlier is None else earlier.shape[0]
    held = (before + rows) // ROWS
    count = n_a + n_b

    def kernel(*refs):
        wg, wu = refs[:2]
        ins_a, ins_b = refs[2 : 2 + na], refs[2 + na : 2 + na + nb]
        outs, total = refs[2 + na + nb + (before > 0) : -1], refs[-1]
        j = pl.program_id(0)

        def product(ins):
            acc = None
            for plane, weight in ((1, wg), (2, wu)):
                left = jnp.concatenate([r[plane] for r in ins], axis=0)
                more = lax.dot_general(
                    left, weight[...], (((1,), (1,)), ((), ())), preferred_element_type=F32
                )
                acc = more if acc is None else acc + more
            return acc

        @pl.when(j == 0)
        def _():
            total[...] = product(ins_a)

        @pl.when(jnp.logical_and(j > 0, j < n_a))
        def _():
            total[...] += product(ins_a)

        @pl.when(j >= n_a)
        def _():
            total[...] += product(ins_b)

        @pl.when(j == count - 1)
        def _():
            if not final:
                outs[0][...] = total[...].astype(BF16)
                return
            for i in range(held):
                for p in range(8):
                    lo = i * ROWS + p * PART
                    if lo < before:
                        value = refs[2 + na + nb][lo : lo + PART]
                    else:
                        value = total[lo - before : lo - before + PART].astype(BF16)
                    outs[p % 4][p // 4, i * PART : (i + 1) * PART] = value

    in_specs = [pl.BlockSpec((depth, TILE), lambda j: (0, j))] * 2
    in_specs += [
        pl.BlockSpec((3, p.shape[1], TILE), lambda j: (0, 0, jnp.minimum(j, n_a - 1)))
        for p in parts_a
    ]
    in_specs += [
        pl.BlockSpec((3, p.shape[1], TILE), lambda j: (0, 0, jnp.maximum(j - n_a, 0)))
        for p in parts_b
    ]
    args = (*weights, *parts_a, *parts_b)
    if before:
        in_specs.append(pl.BlockSpec(earlier.shape, lambda j: (0, 0)))
        args = (*args, earlier)
    if final:
        lengths = (2, held * PART, depth)
        out_shape = [jax.ShapeDtypeStruct(lengths, BF16)] * 4
        out_specs = [pl.BlockSpec(lengths, lambda j: (0, 0, 0))] * 4
    else:
        out_shape = [jax.ShapeDtypeStruct((rows, depth), BF16)]
        out_specs = [pl.BlockSpec((rows, depth), lambda j: (0, 0))]
    return pl.pallas_call(
        kernel,
        out_shape=out_shape,
        grid=(count,),
        in_specs=in_specs,
        out_specs=out_specs,
        scratch_shapes=[pltpu.VMEM((rows, depth), F32)],
        cost_estimate=pl.CostEstimate(
            flops=2 * rows * depth * 2 * count * TILE,
            bytes_accessed=2 * 2 * count * TILE * (depth + rows),
            transcendentals=0,
        ),
        compiler_params=ROOM,
    )(*args)


def to_other(v, a, b):
    pairs = [
        (s * 8 + o * 4 + i, (1 - s) * 8 + (o ^ a) * 4 + (i + b) % 4)
        for s in range(2)
        for o in range(2)
        for i in range(4)
    ]
    return lax.ppermute(v, ("section", "tp"), pairs)


def summed_in_steps(v):
    parts = [along_ring(v[b], "tp", b) for b in (1, 2, 3)]
    sums = [added(v[0][a], *(p[a] for p in parts)).astype(BF16) for a in range(2)]
    return [to_other(sums[a], a, 0) for a in range(2)]


def finished(main, tail, taken, rest, cot, owner):
    depth = cot.shape[1]
    parts = (*main, *tail)

    def kernel(own_ref, *refs):
        cot_ref, out, total = refs[-3:]
        for group, blocks in ((refs[: len(main)], taken), (refs[len(main) : -3], rest)):
            for i, b in enumerate(blocks):
                at = pl.ds(pl.multiple_of(own_ref[b] * PART, PART), PART)
                acc = cot_ref[at].astype(F32)
                for ref in group:
                    acc = acc + ref[i * PART : (i + 1) * PART].astype(F32)
                total[at] = acc
        out[...] = total[...].T.astype(BF16)

    return pl.pallas_call(
        kernel,
        out_shape=jax.ShapeDtypeStruct((depth, ROWS), BF16),
        grid_spec=pltpu.PrefetchScalarGridSpec(
            num_scalar_prefetch=1,
            grid=(1,),
            in_specs=[pl.BlockSpec(p.shape, lambda j, *_: (0, 0)) for p in (*parts, cot)],
            out_specs=pl.BlockSpec((depth, ROWS), lambda j, *_: (0, 0)),
            scratch_shapes=[pltpu.VMEM((ROWS, depth), F32)],
        ),
        cost_estimate=pl.CostEstimate(
            flops=9 * ROWS * depth, bytes_accessed=20 * ROWS * depth, transcendentals=0
        ),
        compiler_params=ROOM,
        name="finish",
    )(owner, *parts, cot)


def layers_back(normed, cotangent, w_gate, w_up, w_down):
    weights = (w_gate[0], w_up[0], w_down[0])
    columns = weights[0].shape[1]
    tiles = columns // TILE
    n_a = 5
    n_b = tiles - n_a
    scale = 1.0 / math.sqrt(8 * ROWS)

    me_f = lax.axis_index("fsdp")
    zh, y = me_f // 4, me_f % 4
    steps = jnp.arange(8, dtype=jnp.int32)
    turn = steps // 2 + steps // 4 - 2 * (steps // 6)
    owner = ((zh + steps % 2) % 2) * 4 + (y + turn) % 4 + held(weights[1:])
    own, cot_own = stacked(normed[0].T, cotangent[0].T)
    pieces = gathered(own)
    cot_other = to_other(cot_own, 0, 0)
    first, rest = range(6, 8), range(0, 6)
    rows, *b_first = project(pieces, owner, None, weights, first, n_a, n_b, TILE)
    a_first = project(None, None, rows, weights, first, 0, 2, n_a * TILE // 2)
    a_rest = project(None, None, rows, weights, rest, 0, n_a, TILE)
    b_rest = project(None, None, rows, weights, rest, n_a, n_b, TILE)
    sides = flipped(rows)

    def by_step(far, near):
        return [near[0:2], near[2:4], far, near[4:6]]

    a = spread_pair_first(activate(reduced_ring_first(by_step(a_first, a_rest))))
    b = spread_ring_first(activate(reduced_pair_first(by_step(b_first, b_rest))))

    def of(parts, group):
        return flat([parts[i] for i in group])

    def dx(group, earlier, final):
        return input_grad(of(a, group), of(b, group), weights[:2], n_a, n_b, earlier, final)

    groups = (0, 2, 4), (1, 3, 5), (6, 7)
    (part,) = dx(groups[0], None, False)
    main = summed_in_steps(dx(groups[1], part, True))
    sums_a = weight_sums(of(a, range(0, 6)), sides, n_a)
    sums_b = weight_sums(of(b, range(0, 5)), sides, n_b)
    tail = summed_in_steps(dx(groups[2], None, True))
    grads = weight_grads(of(a, range(6, 8)), sides, sums_a, 0, n_a, columns, scale, None)
    grads = weight_grads(of(b, range(5, 8)), sides, sums_b, n_a, n_b, columns, scale, grads)
    passed = finished(main, tail, groups[0] + groups[1], groups[2], cot_other, owner)
    return (passed.T[None], grads[0][None], grads[1][None], grads[2][None])


def solution(mesh):
    acts = P("section", "tp", "fsdp")
    weights = P("section", "fsdp", "tp")
    return jax.shard_map(
        layers_back,
        mesh=mesh,
        in_specs=(acts, acts, weights, weights, weights),
        out_specs=(acts, weights, weights, weights),
        check_vma=False,
    )
```

time: 591 us -> 263 us (0.45)
  waiting for transfers between devices: 456 us -> 117 us
  starting transfers between devices: 5.38 us -> 80.2 us
  Pallas kernels: 0 us -> 55.4 us
  matrix products: 50.6 us -> 0 us
  blocking collectives: 34.9 us -> 0 us
  other arithmetic: 27.1 us -> 4.18 us
  between operations: 14.1 us -> 1.03 us
    reduce_scatter x1 -> x0, waiting for transfers between devices: 293 us -> none  [local(): lax.psum_scatter(jnp.concatenate((gate, up, back), axis=1), 'fsdp', scatt...]
    all_gather x1 -> x0, waiting for transfers between devices: 160 us -> none  [in_one_piece(): lax.all_gather(both, axis, axis=dim, tiled=True)]
    ppermute x1 -> x52, waiting for transfers between devices: 0.01 us -> 117 us  [the longest x34 81.3 us: along_ring(): return lax.ppermute(v, axis, pairs)]
    ppermute x1 -> x52, starting transfers between devices: 0.86 us -> 80.2 us  [the longest x34 40.5 us: along_ring(): return lax.ppermute(v, axis, pairs)]
    pallas_call x0 -> x15, Pallas kernels: none -> 55.4 us  [the longest x4 17.5 us: project(): pl.pallas_call(kernel, out_shape=out_shape, grid_spec=pltpu.PrefetchScala...]
    dot_general x8 -> x0, matrix products: 50.6 us -> none  [the longest x3 21.6 us: column_grad(): lax.dot_general(left, right, (((0,), (0,)), ((), ())), preferred_element_...]
    all_to_all x1 -> x0, blocking collectives: 34.9 us -> none  [from_everyone(): return lax.all_to_all(copies, axis, split_axis=0, concat_axis=0, tiled=True)]
    concatenate x3 -> x0, other arithmetic: 22.7 us -> none  [the longest x1 20.3 us: local(): jnp.concatenate((gate, up, back), axis=1)]
  transfers between devices with their start and end apart: 4 -> 52, of which waited for: 3 -> 15; matrix products, arithmetic and copies ran while one was open for 4% -> 2% of each run, Pallas kernels for 0% -> 19%
where the time goes in v1:
time: 263 us
  waiting for transfers between devices  117 us (44%)
  starting transfers between devices  80.2 us (30%)
  Pallas kernels  55.4 us (21%)
  local copies, waits for them, and re-layouts  5.44 us (2%)
  other arithmetic  4.18 us (2%)
    ppermute x34, waiting for transfers between devices, along_ring(): return lax.ppermute(v, axis, pairs)  81.3 us
    ppermute x34, starting transfers between devices, along_ring(): return lax.ppermute(v, axis, pairs)  40.5 us
    ppermute x13, waiting for transfers between devices, across(): return lax.ppermute(v, axis, [(i, (i + 4) % 8) for i in range(8)])  35.6 us
    ppermute x13, starting transfers between devices, across(): return lax.ppermute(v, axis, [(i, (i + 4) % 8) for i in range(8)])  22.3 us
    pallas_call x4, Pallas kernels, project(): pl.pallas_call(kernel, out_shape=out_shape, grid_spec=pltpu.PrefetchScala...  17.5 us
    ppermute x5, starting transfers between devices, to_other(): return lax.ppermute(v, ('section', 'tp'), pairs)  17.4 us
    pallas_call x3, Pallas kernels, input_grad(): pl.pallas_call(kernel, out_shape=out_shape, grid=(count,), in_specs=in_sp...  16.8 us
    pallas_call x2, Pallas kernels, weight_sums(): pl.pallas_call(kernel, out_shape=[jax.ShapeDtypeStruct((depth, count * TI...  9.83 us
  transfers between devices with their start and end apart: 52, of which 15 were waited for; matrix products, arithmetic and copies ran while one was open for 2% of the time, Pallas kernels for 19%

profile of v1, /device:TPU:1, one launch (start us, length us, event | category | flops | bytes accessed | tf_op | source)
XLA Modules:
  0.0 263.1 jit_solution(10592051168453687902)
XLA Ops:
  7.8 5.2 %collective-permute-done.1.refs_4_ = bf16[2,128,576]{2,1,0:T(8,128)(2,1)S(1)} collective-permute-done((bf16[2,128,576]{2,1,0:T(8,128)(2,1)S(1)}, bf16[2,128,576]{2,1,0:T(8,128)(2,1)S(1)}, u32[]{:S(2)}, u32[]{:S(2)}) %collective-permute-start.1) | collective-permute-done | bytes 294944 | tf_op jit(solution)/shard_map/ppermute | solution.py:21
  13.4 2.5 collective-permute-start.3
  15.9 2.7 %collective-permute-start.5 = (bf16[2,128,576]{2,1,0:T(8,128)(2,1)S(1)}, bf16[2,128,576]{2,1,0:T(8,128)(2,1)S(1)}, u32[]{:S(2)}, u32[]{:S(2)}) collective-permute-start(bf16[2,128,576]{2,1,0:T(8,128)(2,1)S(1)} %collective-permute-done.4.refs_5_), channel_id=1, source_target_pairs={{0,24},{8,0},{16,8},{24,16},{32,56},{40,32},{48,40},{56,48},{1,25}... | collective-permute-start | bytes 884744 | tf_op jit(solution)/shard_map/ppermute | solution.py:21
  26.3 3.2 %shard_map.84 = (bf16[2,1024,576]{2,1,0:T(8,128)(2,1)S(1)}, bf16[3,128,1024]{2,1,0:T(8,128)(2,1)S(1)}, bf16[3,128,1024]{2,1,0:T(8,128)(2,1)S(1)}) custom-call(s32[8]{0:T(128)S(1)} %fusion.19.refs_0_.own_ref, bf16[2,128,576]{2,1,0:T(8,128)(2,1)S(1)} %get-tuple-element.43.refs_1_, bf16[2,128,576]{2,1,0:T(8,128)(2,1)S(1)} %collective-permute-done.refs_2_, ...), custom_call_target="tpu_custom_call" | custom-call | flops 905969664 | bytes 5111808 | tf_op jit(solution)/shard_map/pallas_call | solution.py:105
  29.5 3.9 %collective-permute-start.22 = (bf16[3,128,1024]{2,1,0:T(8,128)(2,1)S(1)}, bf16[3,128,1024]{2,1,0:T(8,128)(2,1)S(1)}, u32[]{:S(2)}, u32[]{:S(2)}) collective-permute-start(bf16[3,128,1024]{2,1,0:T(8,128)(2,1)S(1)} %get-tuple-element.60), channel_id=1, source_target_pairs={{0,4},{1,5},{2,6},{3,7},{4,0},{5,1},{6,2},{7,3},{8,12},{9,13},{10,... | collective-permute-start | bytes 2359304 | tf_op jit(solution)/shard_map/ppermute | solution.py:25
  33.4 2.9 %shard_map.86 = (bf16[3,128,1280]{2,1,0:T(8,128)(2,1)S(1)}, bf16[3,128,1280]{2,1,0:T(8,128)(2,1)S(1)}) custom-call(bf16[2,1024,576]{2,1,0:T(8,128)(2,1)S(1)} %get-tuple-element.44.refs_0_.rows_ref, bf16[576,2304]{1,0:T(8,128)(2,1)S(1)} %bitcast.32, bf16[576,2304]{1,0:T(8,128)(2,1)S(1)} %bitcast.25, bf16[576,2304]{1,0:T(8,128)(2,1)S(1)} %bitcast.40), custom_call_target="tpu_custom_call" | custom-call | flops 1132462080 | bytes 6389760 | tf_op jit(solution)/shard_map/pallas_call | solution.py:105
  39.1 6.2 %shard_map.85 = (bf16[3,128,1280]{2,1,0:T(8,128)(2,1)S(1)}, bf16[3,128,1280]{2,1,0:T(8,128)(2,1)S(1)}, bf16[3,128,1280]{2,1,0:T(8,128)(2,1)S(1)}, bf16[3,128,128...) custom-call(bf16[2,1024,576]{2,1,0:T(8,128)(2,1)S(1)} %get-tuple-element.44.refs_0_.rows_re, ...), custom_call_target="tpu_custom_call" | custom-call | flops 3397386240 | bytes 10321920 | tf_op jit(solution)/shard_map/pallas_call | solution.py:105
  45.3 5.3 %shard_map.87 = (bf16[3,128,1024]{2,1,0:T(8,128)(2,1)S(1)}, bf16[3,128,1024]{2,1,0:T(8,128)(2,1)S(1)}, bf16[3,128,1024]{2,1,0:T(8,128)(2,1)S(1)}, bf16[3,128,102...) custom-call(bf16[2,1024,576]{2,1,0:T(8,128)(2,1)S(1)} %get-tuple-element.44.refs_0_.rows_re, ...), custom_call_target="tpu_custom_call" | custom-call | flops 2717908992 | bytes 8257536 | tf_op jit(solution)/shard_map/pallas_call | solution.py:105
  50.8 2.9 %collective-permute-start.21 = (bf16[3,128,1024]{2,1,0:T(8,128)(2,1)S(1)}, bf16[3,128,1024]{2,1,0:T(8,128)(2,1)S(1)}, u32[]{:S(2)}, u32[]{:S(2)}) collective-permute-start(bf16[3,128,1024]{2,1,0:T(8,128)(2,1)S(1)} %get-tuple-element.58), channel_id=1, source_target_pairs={{0,4},{1,5},{2,6},{3,7},{4,0},{5,1},{6,2},{7,3},{8,12},{9,13},{10,... | collective-permute-start | bytes 2359304 | tf_op jit(solution)/shard_map/ppermute | solution.py:25
  57.8 9.7 %collective-permute-done.19 = bf16[3,128,1024]{2,1,0:T(8,128)(2,1)S(1)} collective-permute-done((bf16[3,128,1024]{2,1,0:T(8,128)(2,1)S(1)}, bf16[3,128,1024]{2,1,0:T(8,128)(2,1)S(1)}, u32[]{:S(2)}, u32[]{:S(2)}) %collective-permute-start.19) | collective-permute-done | bytes 786464 | tf_op jit(solution)/shard_map/ppermute | solution.py:25
  69.2 17.5 %collective-permute-done.26 = bf16[3,64,1024]{2,1,0:T(8,128)(2,1)S(1)} collective-permute-done((bf16[3,64,1024]{2,1,0:T(8,128)(2,1)S(1)}, bf16[3,64,1024]{2,1,0:T(8,128)(2,1)S(1)}, u32[]{:S(2)}, u32[]{:S(2)}) %collective-permute-start.26) | collective-permute-done | bytes 393248 | tf_op jit(solution)/shard_map/ppermute | solution.py:21
  87.4 3.1 %collective-permute-start.20 = (bf16[3,64,1024]{2,1,0:T(8,128)(2,1)S(1)}, bf16[3,64,1024]{2,1,0:T(8,128)(2,1)S(1)}, u32[]{:S(2)}, u32[]{:S(2)}) collective-permute-start(bf16[3,64,1024]{2,1,0:T(8,128)(2,1)S(1)} %get-tuple-element.88), channel_id=1, source_target_pairs={{0,3},{1,0},{2,1},{3,2},{4,7},{5,4},{6,5},{7,6},{8,11},{9,8},{10,9... | collective-permute-start | bytes 1179656 | tf_op jit(solution)/shard_map/ppermute | solution.py:21
  96.1 7.0 %collective-permute-done.27 = bf16[3,64,1024]{2,1,0:T(8,128)(2,1)S(1)} collective-permute-done((bf16[3,64,1024]{2,1,0:T(8,128)(2,1)S(1)}, bf16[3,64,1024]{2,1,0:T(8,128)(2,1)S(1)}, u32[]{:S(2)}, u32[]{:S(2)}) %collective-permute-start.27) | collective-permute-done | bytes 393248 | tf_op jit(solution)/shard_map/ppermute | solution.py:21
  103.1 3.4 %collective-permute-start.10 = (bf16[3,128,1280]{2,1,0:T(8,128)(2,1)S(1)}, bf16[3,128,1280]{2,1,0:T(8,128)(2,1)S(1)}, u32[]{:S(2)}, u32[]{:S(2)}) collective-permute-start(bf16[3,128,1280]{2,1,0:T(8,128)(2,1)S(1)} %add_convert_fusion.2), channel_id=1, source_target_pairs={{0,3},{1,0},{2,1},{3,2},{4,7},{5,4},{6,5},{7,6},{8,11},{9,8},{10,9... | collective-permute-start | bytes 2949128 | tf_op jit(solution)/shard_map/ppermute | solution.py:21
  110.1 17.1 %collective-permute-done.8 = bf16[3,128,1280]{2,1,0:T(8,128)(2,1)S(1)} collective-permute-done((bf16[3,128,1280]{2,1,0:T(8,128)(2,1)S(1)}, bf16[3,128,1280]{2,1,0:T(8,128)(2,1)S(1)}, u32[]{:S(2)}, u32[]{:S(2)}) %collective-permute-start.8) | collective-permute-done | bytes 983072 | tf_op jit(solution)/shard_map/ppermute | solution.py:21
  131.4 12.7 %collective-permute-done.31.refs_7_.refs_4_ = bf16[3,128,1024]{2,1,0:T(8,128)(2,1)S(1)} collective-permute-done((bf16[3,128,1024]{2,1,0:T(8,128)(2,1)S(1)}, bf16[3,128,1024]{2,1,0:T(8,128)(2,1)S(1)}, u32[]{:S(2)}, u32[]{:S(2)}) %collective-permute-start.31) | collective-permute-done | bytes 786464 | tf_op jit(solution)/shard_map/ppermute | solution.py:21
  148.9 9.4 %collective-permute-done.28.refs_5_.refs_1_ = bf16[3,128,1024]{2,1,0:T(8,128)(2,1)S(1)} collective-permute-done((bf16[3,128,1024]{2,1,0:T(8,128)(2,1)S(1)}, bf16[3,128,1024]{2,1,0:T(8,128)(2,1)S(1)}, u32[]{:S(2)}, u32[]{:S(2)}) %collective-permute-start.28) | collective-permute-done | bytes 786464 | tf_op jit(solution)/shard_map/ppermute | solution.py:25
  159.3 15.9 %collective-permute-done.32.refs_7_.refs_3_ = bf16[3,128,1024]{2,1,0:T(8,128)(2,1)S(1)} collective-permute-done((bf16[3,128,1024]{2,1,0:T(8,128)(2,1)S(1)}, bf16[3,128,1024]{2,1,0:T(8,128)(2,1)S(1)}, u32[]{:S(2)}, u32[]{:S(2)}) %collective-permute-start.32) | collective-permute-done | bytes 786464 | tf_op jit(solution)/shard_map/ppermute | solution.py:25
  179.0 9.1 %collective-permute-done.16.refs_3_ = bf16[3,128,1280]{2,1,0:T(8,128)(2,1)S(1)} collective-permute-done((bf16[3,128,1280]{2,1,0:T(8,128)(2,1)S(1)}, bf16[3,128,1280]{2,1,0:T(8,128)(2,1)S(1)}, u32[]{:S(2)}, u32[]{:S(2)}) %collective-permute-start.16) | collective-permute-done | bytes 983072 | tf_op jit(solution)/shard_map/ppermute | solution.py:21
  189.1 5.9 %shard_map.88.refs_8_ = bf16[384,576]{1,0:T(8,128)(2,1)S(1)} custom-call(bf16[576,2304]{1,0:T(8,128)(2,1)S(1)} %bitcast.35, bf16[576,2304]{1,0:T(8,128)(2,1)S(1)} %bitcast.28, bf16[3,128,1280]{2,1,0:T(8,128)(2,1)S(1)} %pad_maximum_fusion.refs_2_.refs_0_, bf16[3,128,1280]{2,1,0:T(8,128)(2,1)S(1)} %collective-permute-done.33.refs_3_.refs_2_, ...), custom_call_target="tpu_custom_call" | custom-call | flops 2038431744 | bytes 8847360 | tf_op jit(solution)/shard_map/pallas_call | solution.py:363
  195.5 6.0 %shard_map.89 = (bf16[2,96,576]{2,1,0:T(8,128)(2,1)S(1)}, bf16[2,96,576]{2,1,0:T(8,128)(2,1)S(1)}, bf16[2,96,576]{2,1,0:T(8,128)(2,1)S(1)}, bf16[2,96,576]{2,1,0:T(8,128)(2,1)S(1)}) custom-call(bf16[576,2304]{1,0:T(8,128)(2,1)S(1)} %bitcast.36, bf16[576,2304]{1,0:T(8,128)(2,1)S(1)} %bitcast.29, ...), custom_call_target="tpu_custom_call" | custom-call | flops 2038431744 | bytes 8847360 | tf_op jit(solution)/shard_map/pallas_call | solution.py:363
  201.6 3.6 %collective-permute-start.36 = (bf16[2,96,576]{2,1,0:T(8,128)(2,1)S(1)}, bf16[2,96,576]{2,1,0:T(8,128)(2,1)S(1)}, u32[]{:S(2)}, u32[]{:S(2)}) collective-permute-start(bf16[2,96,576]{2,1,0:T(8,128)(2,1)S(1)} %get-tuple-element.63), channel_id=1, source_target_pairs={{0,16},{8,24},{16,0},{24,8},{32,48},{40,56},{48,32},{56,40},{1,17}... | collective-permute-start | bytes 663560 | tf_op jit(solution)/shard_map/ppermute | solution.py:21
  206.0 4.5 %shard_map.91 = (f32[576,1024]{1,0:T(8,128)S(1)}, f32[576,1024]{1,0:T(8,128)S(1)}, f32[576,1024]{1,0:T(8,128)S(1)}) custom-call(bf16[2,576,1024]{2,1,0:T(8,128)(2,1)S(1)} %flip.1.sides_ref, bf16[3,128,1024]{2,1,0:T(8,128)(2,1)S(1)} %pad_maximum_fusion.1.refs_5_.refs_0_, bf16[3,128,1024]{2,1,0:T(8,128)(2,1)S(1)} %collective-permute-done.28.refs_5_.refs_1_, ...), custom_call_target="tpu_custom_call" | custom-call | flops 2264924160 | bytes 11010048 | tf_op jit(solution)/shard_map/pallas_call | solution.py:248
  210.5 6.3 %collective-permute-done.43.refs_5_ = bf16[3,64,1024]{2,1,0:T(8,128)(2,1)S(1)} collective-permute-done((bf16[3,64,1024]{2,1,0:T(8,128)(2,1)S(1)}, bf16[3,64,1024]{2,1,0:T(8,128)(2,1)S(1)}, u32[]{:S(2)}, u32[]{:S(2)}) %collective-permute-start.43) | collective-permute-done | bytes 393248 | tf_op jit(solution)/shard_map/ppermute | solution.py:21
  219.8 2.6 collective-permute-start.37
  222.4 5.3 %shard_map.92 = (f32[576,1280]{1,0:T(8,128)S(1)}, f32[576,1280]{1,0:T(8,128)S(1)}, f32[576,1280]{1,0:T(8,128)S(1)}) custom-call(bf16[2,576,1024]{2,1,0:T(8,128)(2,1)S(1)} %flip.1.sides_ref, bf16[3,128,1280]{2,1,0:T(8,128)(2,1)S(1)} %pad_maximum_fusion.refs_2_.refs_0_, bf16[3,128,1280]{2,1,0:T(8,128)(2,1)S(1)} %collective-permute-done.15.refs_2_.refs_1_, ...), custom_call_target="tpu_custom_call" | custom-call | flops 3397386240 | bytes 14745600 | tf_op jit(solution)/shard_map/pallas_call | solution.py:248
  227.8 12.1 %collective-permute-start.51 = (bf16[128,576]{1,0:T(8,128)(2,1)S(1)}, bf16[128,576]{1,0:T(8,128)(2,1)S(1)}, u32[]{:S(2)}, u32[]{:S(2)}) collective-permute-start(bf16[128,576]{1,0:T(8,128)(2,1)S(1)} %get-tuple-element.69), channel_id=1, source_target_pairs={{0,64},{8,72},{16,80},{24,88},{32,96},{40,104},{48,112},{56,120},{... | collective-permute-start | bytes 442376 | tf_op jit(solution)/shard_map/ppermute | solution.py:386
  240.9 4.9 %shard_map.90 = (bf16[2,32,576]{2,1,0:T(8,128)(2,1)S(1)}, bf16[2,32,576]{2,1,0:T(8,128)(2,1)S(1)}, bf16[2,32,576]{2,1,0:T(8,128)(2,1)S(1)}, bf16[2,32,576]{2,1,0:T(8,128)(2,1)S(1)}) custom-call(bf16[576,2304]{1,0:T(8,128)(2,1)S(1)} %bitcast.37, bf16[576,2304]{1,0:T(8,128)(2,1)S(1)} %bitcast.30, ...), custom_call_target="tpu_custom_call" | custom-call | flops 1358954496 | bytes 7667712 | tf_op jit(solution)/shard_map/pallas_call | solution.py:363
  245.8 2.9 %collective-permute-start.47 = (bf16[2,32,576]{2,1,0:T(8,128)(2,1)S(1)}, bf16[2,32,576]{2,1,0:T(8,128)(2,1)S(1)}, u32[]{:S(2)}, u32[]{:S(2)}) collective-permute-start(bf16[2,32,576]{2,1,0:T(8,128)(2,1)S(1)} %get-tuple-element.67), channel_id=1, source_target_pairs={{0,16},{8,24},{16,0},{24,8},{32,48},{40,56},{48,32},{56,40},{1,17}... | collective-permute-start | bytes 221192 | tf_op jit(solution)/shard_map/ppermute | solution.py:21
  248.7 4.1 %shard_map.93 = (bf16[576,2304]{1,0:T(8,128)(2,1)}, bf16[576,2304]{1,0:T(8,128)(2,1)}, bf16[576,2304]{1,0:T(8,128)(2,1)}) custom-call(bf16[2,576,1024]{2,1,0:T(8,128)(2,1)S(1)} %flip.1.sides_ref, f32[576,1280]{1,0:T(8,128)S(1)} %get-tuple-element.73.refs_0_, f32[576,1280]{1,0:T(8,128)S(1)} %get-tuple-element.74.refs_1_, ...), custom_call_target="tpu_custom_call" | custom-call | flops 1132462080 | bytes 15237120 | tf_op jit(solution)/shard_map/pallas_call | solution.py:274
  252.8 2.4 collective-permute-start.38
  257.4 4.3 %shard_map.94 = (bf16[576,2304]{1,0:T(8,128)(2,1)}, bf16[576,2304]{1,0:T(8,128)(2,1)}, bf16[576,2304]{1,0:T(8,128)(2,1)}) custom-call(bf16[2,576,1024]{2,1,0:T(8,128)(2,1)S(1)} %flip.1.sides_ref, f32[576,1024]{1,0:T(8,128)S(1)} %get-tuple-element.70.refs_0_, ...), custom_call_target="tpu_custom_call", output_to_operand_aliasing={{0}: (9, {}), {1}: (10, {}), {2}: (11, {})} | custom-call | flops 1358954496 | bytes 12976128 | tf_op jit(solution)/shard_map/pallas_call | solution.py:274
  (122 shorter events, 57.5 us)
Async XLA Ops:
  29.5 24.2 %collective-permute-start.22 = (bf16[3,128,1024]{2,1,0:T(8,128)(2,1)S(1)}, bf16[3,128,1024]{2,1,0:T(8,128)(2,1)S(1)}, u32[]{:S(2)}, u32[]{:S(2)}) collective-permute-start(bf16[3,128,1024]{2,1,0:T(8,128)(2,1)S(1)} %get-tuple-element.60), channel_id=1, source_target_pairs={{0,4},{1,5},{2,6},{3,7},{4,0},{5,1},{6,2},{7,3},{8,12},{9,13},{10,... | collective-permute-start | bytes 2359304 | tf_op jit(solution)/shard_map/ppermute | solution.py:25
  36.2 21.3 %collective-permute-start.12 = (bf16[3,128,1280]{2,1,0:T(8,128)(2,1)S(1)}, bf16[3,128,1280]{2,1,0:T(8,128)(2,1)S(1)}, u32[]{:S(2)}, u32[]{:S(2)}) collective-permute-start(bf16[3,128,1280]{2,1,0:T(8,128)(2,1)S(1)} %get-tuple-element.52), channel_id=1, source_target_pairs={{0,1},{1,2},{2,3},{3,0},{4,5},{5,6},{6,7},{7,4},{8,9},{9,10},{10,1... | collective-permute-start | bytes 2949128 | tf_op jit(solution)/shard_map/ppermute | solution.py:21
  37.6 31.1 %collective-permute-start.9 = (bf16[3,128,1280]{2,1,0:T(8,128)(2,1)S(1)}, bf16[3,128,1280]{2,1,0:T(8,128)(2,1)S(1)}, u32[]{:S(2)}, u32[]{:S(2)}) collective-permute-start(bf16[3,128,1280]{2,1,0:T(8,128)(2,1)S(1)} %get-tuple-element.48), channel_id=1, source_target_pairs={{0,3},{1,0},{2,1},{3,2},{4,7},{5,4},{6,5},{7,6},{8,11},{9,8},{10,9... | collective-permute-start | bytes 2949128 | tf_op jit(solution)/shard_map/ppermute | solution.py:21
  50.6 16.9 %collective-permute-start.19 = (bf16[3,128,1024]{2,1,0:T(8,128)(2,1)S(1)}, bf16[3,128,1024]{2,1,0:T(8,128)(2,1)S(1)}, u32[]{:S(2)}, u32[]{:S(2)}) collective-permute-start(bf16[3,128,1024]{2,1,0:T(8,128)(2,1)S(1)} %get-tuple-element.56), channel_id=1, source_target_pairs={{0,4},{1,5},{2,6},{3,7},{4,0},{5,1},{6,2},{7,3},{8,12},{9,13},{10,... | collective-permute-start | bytes 2359304 | tf_op jit(solution)/shard_map/ppermute | solution.py:25
  50.8 36.7 %collective-permute-start.21 = (bf16[3,128,1024]{2,1,0:T(8,128)(2,1)S(1)}, bf16[3,128,1024]{2,1,0:T(8,128)(2,1)S(1)}, u32[]{:S(2)}, u32[]{:S(2)}) collective-permute-start(bf16[3,128,1024]{2,1,0:T(8,128)(2,1)S(1)} %get-tuple-element.58), channel_id=1, source_target_pairs={{0,4},{1,5},{2,6},{3,7},{4,0},{5,1},{6,2},{7,3},{8,12},{9,13},{10,... | collective-permute-start | bytes 2359304 | tf_op jit(solution)/shard_map/ppermute | solution.py:25
  53.7 37.3 %collective-permute-start.11 = (bf16[3,128,1280]{2,1,0:T(8,128)(2,1)S(1)}, bf16[3,128,1280]{2,1,0:T(8,128)(2,1)S(1)}, u32[]{:S(2)}, u32[]{:S(2)}) collective-permute-start(bf16[3,128,1280]{2,1,0:T(8,128)(2,1)S(1)} %get-tuple-element.50), channel_id=1, source_target_pairs={{0,3},{1,0},{2,1},{3,2},{4,7},{5,4},{6,5},{7,6},{8,11},{9,8},{10,9... | collective-permute-start | bytes 2949128 | tf_op jit(solution)/shard_map/ppermute | solution.py:21
  57.6 33.0 %collective-permute-start.23 = (bf16[3,64,1024]{2,1,0:T(8,128)(2,1)S(1)}, bf16[3,64,1024]{2,1,0:T(8,128)(2,1)S(1)}, u32[]{:S(2)}, u32[]{:S(2)}) collective-permute-start(bf16[3,64,1024]{2,1,0:T(8,128)(2,1)S(1)} %get-tuple-element.92), channel_id=1, source_target_pairs={{0,1},{1,2},{2,3},{3,0},{4,5},{5,6},{6,7},{7,4},{8,9},{9,10},{10,1... | collective-permute-start | bytes 1179656 | tf_op jit(solution)/shard_map/ppermute | solution.py:21
  67.5 19.2 %collective-permute-start.26 = (bf16[3,64,1024]{2,1,0:T(8,128)(2,1)S(1)}, bf16[3,64,1024]{2,1,0:T(8,128)(2,1)S(1)}, u32[]{:S(2)}, u32[]{:S(2)}) collective-permute-start(bf16[3,64,1024]{2,1,0:T(8,128)(2,1)S(1)} %get-tuple-element.93), channel_id=1, source_target_pairs={{0,3},{1,0},{2,1},{3,2},{4,7},{5,4},{6,5},{7,6},{8,11},{9,8},{10,9... | collective-permute-start | bytes 1179656 | tf_op jit(solution)/shard_map/ppermute | solution.py:21
  68.7 23.7 %collective-permute-start.13 = (bf16[3,128,1280]{2,1,0:T(8,128)(2,1)S(1)}, bf16[3,128,1280]{2,1,0:T(8,128)(2,1)S(1)}, u32[]{:S(2)}, u32[]{:S(2)}) collective-permute-start(bf16[3,128,1280]{2,1,0:T(8,128)(2,1)S(1)} %add_convert_fusion.1), channel_id=1, source_target_pairs={{0,1},{1,2},{2,3},{3,0},{4,5},{5,6},{6,7},{7,4},{8,9},{9,10},{10,1... | collective-permute-start | bytes 2949128 | tf_op jit(solution)/shard_map/ppermute | solution.py:21
  86.7 22.3 %collective-permute-start.18 = (bf16[3,128,1024]{2,1,0:T(8,128)(2,1)S(1)}, bf16[3,128,1024]{2,1,0:T(8,128)(2,1)S(1)}, u32[]{:S(2)}, u32[]{:S(2)}) collective-permute-start(bf16[3,128,1024]{2,1,0:T(8,128)(2,1)S(1)} %get-tuple-element.54), channel_id=1, source_target_pairs={{0,4},{1,5},{2,6},{3,7},{4,0},{5,1},{6,2},{7,3},{8,12},{9,13},{10,... | collective-permute-start | bytes 2359304 | tf_op jit(solution)/shard_map/ppermute | solution.py:25
  92.4 16.5 %collective-permute-start.25 = (bf16[3,64,1024]{2,1,0:T(8,128)(2,1)S(1)}, bf16[3,64,1024]{2,1,0:T(8,128)(2,1)S(1)}, u32[]{:S(2)}, u32[]{:S(2)}) collective-permute-start(bf16[3,64,1024]{2,1,0:T(8,128)(2,1)S(1)} %get-tuple-element.91), channel_id=1, source_target_pairs={{0,1},{1,2},{2,3},{3,0},{4,5},{5,6},{6,7},{7,4},{8,9},{9,10},{10,1... | collective-permute-start | bytes 1179656 | tf_op jit(solution)/shard_map/ppermute | solution.py:21
  95.3 32.0 %collective-permute-start.8 = (bf16[3,128,1280]{2,1,0:T(8,128)(2,1)S(1)}, bf16[3,128,1280]{2,1,0:T(8,128)(2,1)S(1)}, u32[]{:S(2)}, u32[]{:S(2)}) collective-permute-start(bf16[3,128,1280]{2,1,0:T(8,128)(2,1)S(1)} %get-tuple-element.46), channel_id=1, source_target_pairs={{0,1},{1,2},{2,3},{3,0},{4,5},{5,6},{6,7},{7,4},{8,9},{9,10},{10,1... | collective-permute-start | bytes 2949128 | tf_op jit(solution)/shard_map/ppermute | solution.py:21
  103.1 24.2 %collective-permute-start.10 = (bf16[3,128,1280]{2,1,0:T(8,128)(2,1)S(1)}, bf16[3,128,1280]{2,1,0:T(8,128)(2,1)S(1)}, u32[]{:S(2)}, u32[]{:S(2)}) collective-permute-start(bf16[3,128,1280]{2,1,0:T(8,128)(2,1)S(1)} %add_convert_fusion.2), channel_id=1, source_target_pairs={{0,3},{1,0},{2,1},{3,2},{4,7},{5,4},{6,5},{7,6},{8,11},{9,8},{10,9... | collective-permute-start | bytes 2949128 | tf_op jit(solution)/shard_map/ppermute | solution.py:21
  106.5 20.8 %collective-permute-start.14 = (bf16[3,128,1280]{2,1,0:T(8,128)(2,1)S(1)}, bf16[3,128,1280]{2,1,0:T(8,128)(2,1)S(1)}, u32[]{:S(2)}, u32[]{:S(2)}) collective-permute-start(bf16[3,128,1280]{2,1,0:T(8,128)(2,1)S(1)} %add_convert_fusion), channel_id=1, source_target_pairs={{0,4},{1,5},{2,6},{3,7},{4,0},{5,1},{6,2},{7,3},{8,12},{9,13},{10,... | collective-permute-start | bytes 2949128 | tf_op jit(solution)/shard_map/ppermute | solution.py:25
  110.0 34.1 %collective-permute-start.31 = (bf16[3,128,1024]{2,1,0:T(8,128)(2,1)S(1)}, bf16[3,128,1024]{2,1,0:T(8,128)(2,1)S(1)}, u32[]{:S(2)}, u32[]{:S(2)}) collective-permute-start(bf16[3,128,1024]{2,1,0:T(8,128)(2,1)S(1)} %pad_maximum_fusion.1.refs_5_.refs_0_), channel_id=1, source_target_pairs={{0,1},{1,2},{2,3},{3,0},{4,5},{5,6},{6,7},{7,4},{8,9},{9,10},{10,1... | collective-permute-start | bytes 2359304 | tf_op jit(solution)/shard_map/ppermute | solution.py:21
  128.3 20.5 %collective-permute-start.15 = (bf16[3,128,1280]{2,1,0:T(8,128)(2,1)S(1)}, bf16[3,128,1280]{2,1,0:T(8,128)(2,1)S(1)}, u32[]{:S(2)}, u32[]{:S(2)}) collective-permute-start(bf16[3,128,1280]{2,1,0:T(8,128)(2,1)S(1)} %pad_maximum_fusion.refs_2_.refs_0_), channel_id=1, source_target_pairs={{0,4},{1,5},{2,6},{3,7},{4,0},{5,1},{6,2},{7,3},{8,12},{9,13},{10,... | collective-permute-start | bytes 2949128 | tf_op jit(solution)/shard_map/ppermute | solution.py:25
  130.5 27.9 %collective-permute-start.28 = (bf16[3,128,1024]{2,1,0:T(8,128)(2,1)S(1)}, bf16[3,128,1024]{2,1,0:T(8,128)(2,1)S(1)}, u32[]{:S(2)}, u32[]{:S(2)}) collective-permute-start(bf16[3,128,1024]{2,1,0:T(8,128)(2,1)S(1)} %pad_maximum_fusion.1.refs_5_.refs_0_), channel_id=1, source_target_pairs={{0,4},{1,5},{2,6},{3,7},{4,0},{5,1},{6,2},{7,3},{8,12},{9,13},{10,... | collective-permute-start | bytes 2359304 | tf_op jit(solution)/shard_map/ppermute | solution.py:25
  144.1 31.1 %collective-permute-start.32 = (bf16[3,128,1024]{2,1,0:T(8,128)(2,1)S(1)}, bf16[3,128,1024]{2,1,0:T(8,128)(2,1)S(1)}, u32[]{:S(2)}, u32[]{:S(2)}) collective-permute-start(bf16[3,128,1024]{2,1,0:T(8,128)(2,1)S(1)} %collective-permute-done.31.refs_7_.refs_4_), channel_id=1, source_target_pairs={{0,4},{1,5},{2,6},{3,7},{4,0},{5,1},{6,2},{7,3},{8,12},{9,13},{10,... | collective-permute-start | bytes 2359304 | tf_op jit(solution)/shard_map/ppermute | solution.py:25
  146.1 29.9 %collective-permute-start.34 = (bf16[3,128,1280]{2,1,0:T(8,128)(2,1)S(1)}, bf16[3,128,1280]{2,1,0:T(8,128)(2,1)S(1)}, u32[]{:S(2)}, u32[]{:S(2)}) collective-permute-start(bf16[3,128,1280]{2,1,0:T(8,128)(2,1)S(1)} %pad_maximum_fusion.refs_2_.refs_0_), channel_id=1, source_target_pairs={{0,1},{1,2},{2,3},{3,0},{4,5},{5,6},{6,7},{7,4},{8,9},{9,10},{10,1... | collective-permute-start | bytes 2949128 | tf_op jit(solution)/shard_map/ppermute | solution.py:21
  146.9 31.2 %collective-permute-start.33 = (bf16[3,128,1280]{2,1,0:T(8,128)(2,1)S(1)}, bf16[3,128,1280]{2,1,0:T(8,128)(2,1)S(1)}, u32[]{:S(2)}, u32[]{:S(2)}) collective-permute-start(bf16[3,128,1280]{2,1,0:T(8,128)(2,1)S(1)} %pad_maximum_fusion.refs_2_.refs_0_), channel_id=1, source_target_pairs={{0,3},{1,0},{2,1},{3,2},{4,7},{5,4},{6,5},{7,6},{8,11},{9,8},{10,9... | collective-permute-start | bytes 2949128 | tf_op jit(solution)/shard_map/ppermute | solution.py:21
  148.8 39.4 %collective-permute-start.16 = (bf16[3,128,1280]{2,1,0:T(8,128)(2,1)S(1)}, bf16[3,128,1280]{2,1,0:T(8,128)(2,1)S(1)}, u32[]{:S(2)}, u32[]{:S(2)}) collective-permute-start(bf16[3,128,1280]{2,1,0:T(8,128)(2,1)S(1)} %collective-permute-done.15.refs_2_.refs_1_), channel_id=1, source_target_pairs={{0,3},{1,0},{2,1},{3,2},{4,7},{5,4},{6,5},{7,6},{8,11},{9,8},{10,9... | collective-permute-start | bytes 2949128 | tf_op jit(solution)/shard_map/ppermute | solution.py:21
  158.3 37.2 %collective-permute-start.17 = (bf16[3,128,1280]{2,1,0:T(8,128)(2,1)S(1)}, bf16[3,128,1280]{2,1,0:T(8,128)(2,1)S(1)}, u32[]{:S(2)}, u32[]{:S(2)}) collective-permute-start(bf16[3,128,1280]{2,1,0:T(8,128)(2,1)S(1)} %collective-permute-done.15.refs_2_.refs_1_), channel_id=1, source_target_pairs={{0,1},{1,2},{2,3},{3,0},{4,5},{5,6},{6,7},{7,4},{8,9},{9,10},{10,1... | collective-permute-start | bytes 2949128 | tf_op jit(solution)/shard_map/ppermute | solution.py:21
  175.2 20.4 %collective-permute-start.30 = (bf16[3,128,1024]{2,1,0:T(8,128)(2,1)S(1)}, bf16[3,128,1024]{2,1,0:T(8,128)(2,1)S(1)}, u32[]{:S(2)}, u32[]{:S(2)}) collective-permute-start(bf16[3,128,1024]{2,1,0:T(8,128)(2,1)S(1)} %collective-permute-done.29.refs_6_.refs_2_), channel_id=1, source_target_pairs={{0,4},{1,5},{2,6},{3,7},{4,0},{5,1},{6,2},{7,3},{8,12},{9,13},{10,... | collective-permute-start | bytes 2359304 | tf_op jit(solution)/shard_map/ppermute | solution.py:25
  176.1 25.5 %collective-permute-start.42 = (bf16[3,64,1024]{2,1,0:T(8,128)(2,1)S(1)}, bf16[3,64,1024]{2,1,0:T(8,128)(2,1)S(1)}, u32[]{:S(2)}, u32[]{:S(2)}) collective-permute-start(bf16[3,64,1024]{2,1,0:T(8,128)(2,1)S(1)} %slice.172), channel_id=1, source_target_pairs={{0,1},{1,2},{2,3},{3,0},{4,5},{5,6},{6,7},{7,4},{8,9},{9,10},{10,1... | collective-permute-start | bytes 1179656 | tf_op jit(solution)/shard_map/ppermute | solution.py:21
  178.1 62.8 %collective-permute-start.40 = (bf16[3,128,1280]{2,1,0:T(8,128)(2,1)S(1)}, bf16[3,128,1280]{2,1,0:T(8,128)(2,1)S(1)}, u32[]{:S(2)}, u32[]{:S(2)}) collective-permute-start(bf16[3,128,1280]{2,1,0:T(8,128)(2,1)S(1)} %collective-permute-done.34.refs_4_), channel_id=1, source_target_pairs={{0,1},{1,2},{2,3},{3,0},{4,5},{5,6},{6,7},{7,4},{8,9},{9,10},{10,1... | collective-permute-start | bytes 2949128 | tf_op jit(solution)/shard_map/ppermute | solution.py:21
  188.2 52.7 %collective-permute-start.41 = (bf16[3,128,1280]{2,1,0:T(8,128)(2,1)S(1)}, bf16[3,128,1280]{2,1,0:T(8,128)(2,1)S(1)}, u32[]{:S(2)}, u32[]{:S(2)}) collective-permute-start(bf16[3,128,1280]{2,1,0:T(8,128)(2,1)S(1)} %collective-permute-done.16.refs_3_), channel_id=1, source_target_pairs={{0,3},{1,0},{2,1},{3,2},{4,7},{5,4},{6,5},{7,6},{8,11},{9,8},{10,9... | collective-permute-start | bytes 2949128 | tf_op jit(solution)/shard_map/ppermute | solution.py:21
  195.5 21.3 %collective-permute-start.43 = (bf16[3,64,1024]{2,1,0:T(8,128)(2,1)S(1)}, bf16[3,64,1024]{2,1,0:T(8,128)(2,1)S(1)}, u32[]{:S(2)}, u32[]{:S(2)}) collective-permute-start(bf16[3,64,1024]{2,1,0:T(8,128)(2,1)S(1)} %slice.173), channel_id=1, source_target_pairs={{0,3},{1,0},{2,1},{3,2},{4,7},{5,4},{6,5},{7,6},{8,11},{9,8},{10,9... | collective-permute-start | bytes 1179656 | tf_op jit(solution)/shard_map/ppermute | solution.py:21
  201.6 18.2 %collective-permute-start.36 = (bf16[2,96,576]{2,1,0:T(8,128)(2,1)S(1)}, bf16[2,96,576]{2,1,0:T(8,128)(2,1)S(1)}, u32[]{:S(2)}, u32[]{:S(2)}) collective-permute-start(bf16[2,96,576]{2,1,0:T(8,128)(2,1)S(1)} %get-tuple-element.63), channel_id=1, source_target_pairs={{0,16},{8,24},{16,0},{24,8},{32,48},{40,56},{48,32},{56,40},{1,17}... | collective-permute-start | bytes 663560 | tf_op jit(solution)/shard_map/ppermute | solution.py:21
  216.8 23.3 %collective-permute-start.44 = (bf16[3,64,1024]{2,1,0:T(8,128)(2,1)S(1)}, bf16[3,64,1024]{2,1,0:T(8,128)(2,1)S(1)}, u32[]{:S(2)}, u32[]{:S(2)}) collective-permute-start(bf16[3,64,1024]{2,1,0:T(8,128)(2,1)S(1)} %collective-permute-done.42.refs_4_), channel_id=1, source_target_pairs={{0,4},{1,5},{2,6},{3,7},{4,0},{5,1},{6,2},{7,3},{8,12},{9,13},{10,... | collective-permute-start | bytes 1179656 | tf_op jit(solution)/shard_map/ppermute | solution.py:25
  217.4 23.5 %collective-permute-start.45 = (bf16[3,64,1024]{2,1,0:T(8,128)(2,1)S(1)}, bf16[3,64,1024]{2,1,0:T(8,128)(2,1)S(1)}, u32[]{:S(2)}, u32[]{:S(2)}) collective-permute-start(bf16[3,64,1024]{2,1,0:T(8,128)(2,1)S(1)} %collective-permute-done.43.refs_5_), channel_id=1, source_target_pairs={{0,4},{1,5},{2,6},{3,7},{4,0},{5,1},{6,2},{7,3},{8,12},{9,13},{10,... | collective-permute-start | bytes 1179656 | tf_op jit(solution)/shard_map/ppermute | solution.py:25
  227.8 33.8 %collective-permute-start.51 = (bf16[128,576]{1,0:T(8,128)(2,1)S(1)}, bf16[128,576]{1,0:T(8,128)(2,1)S(1)}, u32[]{:S(2)}, u32[]{:S(2)}) collective-permute-start(bf16[128,576]{1,0:T(8,128)(2,1)S(1)} %get-tuple-element.69), channel_id=1, source_target_pairs={{0,64},{8,72},{16,80},{24,88},{32,96},{40,104},{48,112},{56,120},{... | collective-permute-start | bytes 442376 | tf_op jit(solution)/shard_map/ppermute | solution.py:386
  240.1 21.6 %collective-permute-start.39 = (bf16[96,576]{1,0:T(8,128)(2,1)S(1)}, bf16[96,576]{1,0:T(8,128)(2,1)S(1)}, u32[]{:S(2)}, u32[]{:S(2)}) collective-permute-start(bf16[96,576]{1,0:T(8,128)(2,1)S(1)} %get-tuple-element.94), channel_id=1, source_target_pairs={{0,96},{8,104},{16,112},{24,120},{32,64},{40,72},{48,80},{56,88},{... | collective-permute-start | bytes 331784 | tf_op jit(solution)/shard_map/ppermute | solution.py:386
  (26 other events, 255.6 us)
